TPU v7x, 128 devices: a whole 4x4x4 slice. The times are simulated.
128 devices in a mesh: pa: 8 (over z_lo, y), pb: 16 (over z_hi, x, core).
Axes of the slice: x: 4, y: 4, z: 4 (z_hi: 2, z_lo: 2; z = z_hi * 2 + z_lo), core: 2. Of those that a mesh axis runs over, the one named last changes fastest.
Arguments:
- right_side: float32 [128, 128, 256], P(None, 'pa', 'pb'), may hold values from -6 to 6
- coef_x: float32 [128, 128, 256], P(None, 'pa', 'pb'), may hold values from 0.1 to 4
- coef_y: float32 [128, 128, 256], P(None, 'pa', 'pb'), may hold values from 0.1 to 4
- coef_z: float32 [128, 128, 256], P(None, 'pa', 'pb'), may hold values from 0.1 to 4
Outputs:
- solution_field: float32 [128, 128, 256], P(None, 'pa', 'pb')
- residual: float32 [128, 128, 256], P(None, 'pa', 'pb')
All inputs are finite; a program needn't handle non-finite values.
Results may differ from a plain program's by a relative error of at most 0.0003.
Values sent between devices are 32-bit elements.
A program may use at most 64 MiB of HBM per device.

v0:
```python
import math
import jax
import jax.numpy as jnp
from jax import lax
from jax.sharding import Mesh
from jax.sharding import PartitionSpec as P

ITERS = 4
PA = ("pa_0", "pa_1")
PB = ("pb_0", "pb_1", "pb_2")
PA_PB = ("pa_0", "pa_1", "pb_0", "pb_1", "pb_2")
mass_shift = 0.5
base_coef = 1.0


def padded_2(x, sides, width, wrap):
    edges = {}
    for axis, dim in sides:
        peers, length = (lax.axis_size(axis), x.shape[dim])
        up = [(i, (i + 1) % peers) for i in range(peers if wrap else peers - 1)]
        last = lax.slice_in_dim(x, length - width, length, axis=dim)
        first = lax.slice_in_dim(x, 0, width, axis=dim)
        edges[dim] = (
            lax.ppermute(last, axis, up),
            lax.ppermute(first, axis, [(b, a) for a, b in up]),
        )
    done = []
    for _, dim in sides:
        low, high = edges[dim]
        around = [(width, width) if d in done else (0, 0) for d in range(x.ndim)]
        x = jnp.concatenate([jnp.pad(low, around), x, jnp.pad(high, around)], axis=dim)
        done.append(dim)
    return x


def by_axis(x, axes):
    for axis in axes:
        x = lax.psum(x, axis)
    return x


def shifted(value, axis, steps):
    count = lax.axis_size(axis)
    pairs = [(source, (source + steps) % count) for source in range(count)]
    return lax.ppermute(value, axis, pairs)


def dft_tables(points):
    positions = lax.iota(jnp.int32, points)
    product = positions[:, None] * positions[None, :] % points
    angles = product.astype(jnp.float32) * (2.0 * math.pi / points)
    return (jnp.cos(angles), jnp.sin(angles))


def apply_along(matrix, values, target_dim):
    moved = jnp.tensordot(matrix, values, axes=([1], [target_dim]), precision=lax.Precision.HIGHEST)
    return jnp.moveaxis(moved, 0, target_dim)


def forward_complex(real_part, imag_part, target_dim):
    cosine_table, sine_table = dft_tables(real_part.shape[target_dim])
    new_real = apply_along(cosine_table, real_part, target_dim) + apply_along(
        sine_table, imag_part, target_dim
    )
    new_imag = apply_along(cosine_table, imag_part, target_dim) - apply_along(
        sine_table, real_part, target_dim
    )
    return (new_real, new_imag)


def inverse_complex(real_part, imag_part, target_dim):
    points = real_part.shape[target_dim]
    cosine_table, sine_table = dft_tables(points)
    inverse_scale = 1.0 / points
    new_real = (
        apply_along(cosine_table, real_part, target_dim)
        - apply_along(sine_table, imag_part, target_dim)
    ) * inverse_scale
    new_imag = (
        apply_along(cosine_table, imag_part, target_dim)
        + apply_along(sine_table, real_part, target_dim)
    ) * inverse_scale
    return (new_real, new_imag)


def wave_term(positions, points):
    return 2.0 - 2.0 * jnp.cos(2.0 * math.pi * positions.astype(jnp.float32) / points)


def divide_symbol(real_part, imag_part, starts, totals):
    wave_x = wave_term(starts[0] + lax.iota(jnp.int32, real_part.shape[0]), totals[0])
    wave_y = wave_term(starts[1] + lax.iota(jnp.int32, real_part.shape[1]), totals[1])
    wave_z = wave_term(starts[2] + lax.iota(jnp.int32, real_part.shape[2]), totals[2])
    symbol = mass_shift + base_coef * (
        wave_x[:, None, None] + wave_y[None, :, None] + wave_z[None, None, :]
    )
    return (real_part / symbol, imag_part / symbol)


def precondition(residual):
    count_x, rows_y, rows_z = residual.shape
    groups_a = lax.axis_size(PA)
    groups_b = lax.axis_size(PB)
    total_y = rows_y * groups_a
    total_z = rows_z * groups_b
    cosine_table, sine_table = dft_tables(count_x)
    real_part = apply_along(cosine_table, residual, 0)
    imag_part = -apply_along(sine_table, residual, 0)
    devices = groups_a * groups_b
    planes = count_x // devices

    def to_slab(values):
        arranged = values.reshape(groups_a, groups_b, planes, rows_y, rows_z)
        return arranged.transpose(2, 0, 3, 1, 4).reshape(planes, total_y, total_z)

    def from_slab(values):
        arranged = values.reshape(planes, groups_a, rows_y, groups_b, rows_z)
        return arranged.transpose(1, 3, 0, 2, 4).reshape(devices, planes, rows_y, rows_z)

    stacked_real = real_part.reshape(devices, planes, rows_y, rows_z)
    stacked_imag = imag_part.reshape(devices, planes, rows_y, rows_z)
    stacked_real, stacked_imag = (
        lax.all_to_all(stacked_real, PA_PB, split_axis=0, concat_axis=0, tiled=True),
        lax.all_to_all(stacked_imag, PA_PB, split_axis=0, concat_axis=0, tiled=True),
    )
    real_part = to_slab(stacked_real)
    imag_part = to_slab(stacked_imag)
    real_part, imag_part = forward_complex(real_part, imag_part, 1)
    real_part, imag_part = forward_complex(real_part, imag_part, 2)
    starts = (lax.axis_index(PA_PB) * planes, 0, 0)
    real_part, imag_part = divide_symbol(real_part, imag_part, starts, (count_x, total_y, total_z))
    real_part, imag_part = inverse_complex(real_part, imag_part, 2)
    real_part, imag_part = inverse_complex(real_part, imag_part, 1)
    stacked_real, stacked_imag = (
        lax.all_to_all(from_slab(real_part), PA_PB, split_axis=0, concat_axis=0, tiled=True),
        lax.all_to_all(from_slab(imag_part), PA_PB, split_axis=0, concat_axis=0, tiled=True),
    )
    real_part = stacked_real.reshape(count_x, rows_y, rows_z)
    imag_part = stacked_imag.reshape(count_x, rows_y, rows_z)
    result = apply_along(cosine_table, real_part, 0) - apply_along(sine_table, imag_part, 0)
    return result * (1.0 / count_x)


def operate(grid_field, coefs, lower_coefs):
    padded = padded_2(grid_field, ((PA, 1), (PB, 2)), 1, True)
    result = mass_shift * grid_field
    result = (
        result
        + coefs[0] * (grid_field - jnp.roll(grid_field, -1, 0))
        + lower_coefs[0] * (grid_field - jnp.roll(grid_field, 1, 0))
    )
    result = (
        result
        + coefs[1] * (grid_field - padded[:, 2:, 1:-1])
        + lower_coefs[1] * (grid_field - padded[:, :-2, 1:-1])
    )
    result = (
        result
        + coefs[2] * (grid_field - padded[:, 1:-1, 2:])
        + lower_coefs[2] * (grid_field - padded[:, 1:-1, :-2])
    )
    return result


def fit_sum(residual, precond):
    return by_axis(jnp.sum(residual * precond), PA_PB)


def body(right_side, coef_x, coef_y, coef_z):
    edge_y = shifted(coef_y[:, -1:, :], PA, 1)
    edge_z = shifted(coef_z[:, :, -1:], PB, 1)
    lower_x = jnp.roll(coef_x, 1, 0)
    lower_y = jnp.concatenate([edge_y, coef_y[:, :-1, :]], axis=1)
    lower_z = jnp.concatenate([edge_z, coef_z[:, :, :-1]], axis=2)
    coefs = (coef_x, coef_y, coef_z)
    lower_coefs = (lower_x, lower_y, lower_z)
    solution_field = jnp.zeros_like(right_side)
    residual = right_side
    precond = precondition(residual)
    direction = precond
    fit_now = fit_sum(residual, precond)
    for iteration in range(ITERS):
        image_field = operate(direction, coefs, lower_coefs)
        step_size = fit_now / by_axis(jnp.sum(direction * image_field), PA_PB)
        solution_field = solution_field + step_size * direction
        residual = residual - step_size * image_field
        if iteration + 1 < ITERS:
            precond = precondition(residual)
            fit_next = fit_sum(residual, precond)
            direction = precond + fit_next / fit_now * direction
            fit_now = fit_next
    return (solution_field, residual)


def solution(mesh):
    torus = Mesh(mesh.devices.reshape(2, 4, 2, 4, 2), ("pa_0", "pa_1", "pb_0", "pb_1", "pb_2"))
    in_specs = (P(None, PA, PB), P(None, PA, PB), P(None, PA, PB), P(None, PA, PB))
    out_specs = (P(None, PA, PB), P(None, PA, PB))
    return jax.shard_map(body, mesh=torus, in_specs=in_specs, out_specs=out_specs, check_vma=False)
```

profile of v0, /device:TPU:11, one launch (start us, length us, event | category | flops | bytes accessed | tf_op | source)
XLA Modules:
  0.0 642.0 jit_solution(13919699423586263251)
XLA Ops:
  8.8 9.5 %all-to-all-start = ((f32[128,1,256]{2,1,0:T(1,128)}), f32[128,1,256]{2,1,0:T(1,128)S(1)}, u32[]{:S(2)}, u32[]{:S(2)}) async-start(f32[128,1,256]{2,1,0:T(1,128)} %reshape.614), calls=%async_computation | async-start | bytes 262144 | tf_op jit(solution)/shard_map/all_to_all | solution.py:123
  26.3 6.5 %all-to-all-start.1 = ((f32[128,1,256]{2,1,0:T(1,128)}), f32[128,1,256]{2,1,0:T(1,128)S(1)}, u32[]{:S(2)}, u32[]{:S(2)}) async-start(f32[128,1,256]{2,1,0:T(1,128)} %reshape.616), calls=%async_computation.1 | async-start | bytes 262144 | tf_op jit(solution)/shard_map/all_to_all | solution.py:124
  35.9 4.7 all-to-all-done.1
  59.9 6.3 all-to-all-start.2
  68.4 5.7 all-to-all-done.2
  74.1 6.2 all-to-all-start.3
  82.5 5.7 all-to-all-done.3
  96.3 4.4 all-reduce.12
  100.7 9.6 %all-reduce.9 = (f32[]{:T(128)}, f32[]{:T(128)}) all-reduce(f32[]{:T(128)} %get-tuple-element.12, f32[]{:T(128)} %get-tuple-element.13), channel_id=1, replica_groups=mesh['pa_0'=2,'pa_1'=4,'pb_0'=2,'pb_1'=4,'pb_2'=2] {'pa_1'}, use_global_device_ids=true, to_apply=%region_2.3 | all-reduce | flops 2 | bytes 16 | tf_op jit(solution)/shard_map/psum | solution.py:38
  110.3 5.9 all-reduce.11
  116.2 9.7 %all-reduce.8 = (f32[]{:T(128)}, f32[]{:T(128)}) all-reduce(f32[]{:T(128)} %get-tuple-element.10, f32[]{:T(128)} %get-tuple-element.11), channel_id=1, replica_groups=mesh['pa_0'=2,'pa_1'=4,'pb_0'=2,'pb_1'=4,'pb_2'=2] {'pb_1'}, use_global_device_ids=true, to_apply=%region_4.5 | all-reduce | flops 2 | bytes 16 | tf_op jit(solution)/shard_map/psum | solution.py:38
  125.9 9.5 %all-reduce.10 = (f32[]{:T(128)}, f32[]{:T(128)}) all-reduce(f32[]{:T(128)} %get-tuple-element.4, f32[]{:T(128)} %get-tuple-element.5), channel_id=1, replica_groups=mesh['pa_0'=2,'pa_1'=4,'pb_0'=2,'pb_1'=4,'pb_2'=2] {'pb_2'}, use_global_device_ids=true, to_apply=%region_5.6 | all-reduce | flops 2 | bytes 16 | tf_op jit(solution)/shard_map/psum | solution.py:38
  139.5 7.2 %all-to-all-start.4 = ((f32[128,1,256]{2,1,0:T(1,128)}), f32[128,1,256]{2,1,0:T(1,128)S(1)}, u32[]{:S(2)}, u32[]{:S(2)}) async-start(f32[128,1,256]{2,1,0:T(1,128)} %reshape.622), calls=%async_computation.4 | async-start | bytes 262144 | tf_op jit(solution)/shard_map/all_to_all | solution.py:123
  148.3 6.4 all-to-all-done.4
  154.6 6.5 %all-to-all-start.5 = ((f32[128,1,256]{2,1,0:T(1,128)}), f32[128,1,256]{2,1,0:T(1,128)S(1)}, u32[]{:S(2)}, u32[]{:S(2)}) async-start(f32[128,1,256]{2,1,0:T(1,128)} %reshape.624), calls=%async_computation.5 | async-start | bytes 262144 | tf_op jit(solution)/shard_map/all_to_all | solution.py:124
  163.7 5.2 all-to-all-done.5
  188.3 6.3 all-to-all-start.6
  196.8 5.7 all-to-all-done.6
  202.5 6.2 all-to-all-start.7
  210.9 5.7 all-to-all-done.7
  219.5 4.4 psum.290
  223.8 7.7 %psum.291 = f32[]{:T(128)} all-reduce(f32[]{:T(128)} %psum.290), channel_id=1, replica_groups=mesh['pa_0'=2,'pa_1'=4,'pb_0'=2,'pb_1'=4,'pb_2'=2] {'pa_1'}, use_global_device_ids=true, to_apply=%region_14.15 | all-reduce | flops 1 | bytes 8 | tf_op jit(solution)/shard_map/psum | solution.py:38
  231.6 5.9 psum.292
  237.4 7.7 %psum.293 = f32[]{:T(128)} all-reduce(f32[]{:T(128)} %psum.292), channel_id=1, replica_groups=mesh['pa_0'=2,'pa_1'=4,'pb_0'=2,'pb_1'=4,'pb_2'=2] {'pb_1'}, use_global_device_ids=true, to_apply=%region_16.17 | all-reduce | flops 1 | bytes 8 | tf_op jit(solution)/shard_map/psum | solution.py:38
  245.2 9.8 %psum.294 = f32[]{:T(128)} all-reduce(f32[]{:T(128)} %psum.293), channel_id=1, replica_groups=mesh['pa_0'=2,'pa_1'=4,'pb_0'=2,'pb_1'=4,'pb_2'=2] {'pb_2'}, use_global_device_ids=true, to_apply=%region_17.18 | all-reduce | flops 1 | bytes 8 | tf_op jit(solution)/shard_map/psum | solution.py:38
  261.6 4.4 psum.295
  266.0 9.5 %psum.296 = f32[]{:T(128)} all-reduce(f32[]{:T(128)} %psum.295), channel_id=1, replica_groups=mesh['pa_0'=2,'pa_1'=4,'pb_0'=2,'pb_1'=4,'pb_2'=2] {'pa_1'}, use_global_device_ids=true, to_apply=%region_20.21 | all-reduce | flops 1 | bytes 8 | tf_op jit(solution)/shard_map/psum | solution.py:38
  275.5 5.9 psum.297
  281.4 9.0 %psum.298 = f32[]{:T(128)} all-reduce(f32[]{:T(128)} %psum.297), channel_id=1, replica_groups=mesh['pa_0'=2,'pa_1'=4,'pb_0'=2,'pb_1'=4,'pb_2'=2] {'pb_1'}, use_global_device_ids=true, to_apply=%region_22.23 | all-reduce | flops 1 | bytes 8 | tf_op jit(solution)/shard_map/psum | solution.py:38
  290.4 9.9 %psum.299 = f32[]{:T(128)} all-reduce(f32[]{:T(128)} %psum.298), channel_id=1, replica_groups=mesh['pa_0'=2,'pa_1'=4,'pb_0'=2,'pb_1'=4,'pb_2'=2] {'pb_2'}, use_global_device_ids=true, to_apply=%region_23.24 | all-reduce | flops 1 | bytes 8 | tf_op jit(solution)/shard_map/psum | solution.py:38
  304.3 6.8 %all-to-all-start.8 = ((f32[128,1,256]{2,1,0:T(1,128)}), f32[128,1,256]{2,1,0:T(1,128)S(1)}, u32[]{:S(2)}, u32[]{:S(2)}) async-start(f32[128,1,256]{2,1,0:T(1,128)} %reshape.630), calls=%async_computation.8 | async-start | bytes 262144 | tf_op jit(solution)/shard_map/all_to_all | solution.py:123
  312.7 6.4 all-to-all-done.8
  319.1 7.4 %all-to-all-start.9 = ((f32[128,1,256]{2,1,0:T(1,128)}), f32[128,1,256]{2,1,0:T(1,128)}, u32[]{:S(2)}, u32[]{:S(2)}) async-start(f32[128,1,256]{2,1,0:T(1,128)} %reshape.632), calls=%async_computation.9 | async-start | bytes 262144 | tf_op jit(solution)/shard_map/all_to_all | solution.py:124
  355.2 6.7 %all-to-all-start.10 = ((f32[128,1,256]{2,1,0:T(1,128)}), f32[128,1,256]{2,1,0:T(1,128)S(1)}, u32[]{:S(2)}, u32[]{:S(2)}) async-start(f32[128,1,256]{2,1,0:T(1,128)} %reshape.634), calls=%async_computation.10 | async-start | bytes 262144 | tf_op jit(solution)/shard_map/all_to_all | solution.py:135
  364.1 5.8 all-to-all-done.10
  369.9 6.2 all-to-all-start.11
  378.3 5.7 all-to-all-done.11
  386.9 4.4 psum.300
  391.3 7.7 %psum.301 = f32[]{:T(128)} all-reduce(f32[]{:T(128)} %psum.300), channel_id=1, replica_groups=mesh['pa_0'=2,'pa_1'=4,'pb_0'=2,'pb_1'=4,'pb_2'=2] {'pa_1'}, use_global_device_ids=true, to_apply=%region_26.27 | all-reduce | flops 1 | bytes 8 | tf_op jit(solution)/shard_map/psum | solution.py:38
  399.0 5.9 psum.302
  404.9 7.7 %psum.303 = f32[]{:T(128)} all-reduce(f32[]{:T(128)} %psum.302), channel_id=1, replica_groups=mesh['pa_0'=2,'pa_1'=4,'pb_0'=2,'pb_1'=4,'pb_2'=2] {'pb_1'}, use_global_device_ids=true, to_apply=%region_28.29 | all-reduce | flops 1 | bytes 8 | tf_op jit(solution)/shard_map/psum | solution.py:38
  412.6 9.7 %psum.304 = f32[]{:T(128)} all-reduce(f32[]{:T(128)} %psum.303), channel_id=1, replica_groups=mesh['pa_0'=2,'pa_1'=4,'pb_0'=2,'pb_1'=4,'pb_2'=2] {'pb_2'}, use_global_device_ids=true, to_apply=%region_29.30 | all-reduce | flops 1 | bytes 8 | tf_op jit(solution)/shard_map/psum | solution.py:38
  428.8 4.4 psum.305
  433.2 9.5 %psum.306 = f32[]{:T(128)} all-reduce(f32[]{:T(128)} %psum.305), channel_id=1, replica_groups=mesh['pa_0'=2,'pa_1'=4,'pb_0'=2,'pb_1'=4,'pb_2'=2] {'pa_1'}, use_global_device_ids=true, to_apply=%region_32.33 | all-reduce | flops 1 | bytes 8 | tf_op jit(solution)/shard_map/psum | solution.py:38
  442.8 5.9 psum.307
  448.6 9.0 %psum.308 = f32[]{:T(128)} all-reduce(f32[]{:T(128)} %psum.307), channel_id=1, replica_groups=mesh['pa_0'=2,'pa_1'=4,'pb_0'=2,'pb_1'=4,'pb_2'=2] {'pb_1'}, use_global_device_ids=true, to_apply=%region_34.35 | all-reduce | flops 1 | bytes 8 | tf_op jit(solution)/shard_map/psum | solution.py:38
  457.7 9.9 %psum.309 = f32[]{:T(128)} all-reduce(f32[]{:T(128)} %psum.308), channel_id=1, replica_groups=mesh['pa_0'=2,'pa_1'=4,'pb_0'=2,'pb_1'=4,'pb_2'=2] {'pb_2'}, use_global_device_ids=true, to_apply=%region_35.36 | all-reduce | flops 1 | bytes 8 | tf_op jit(solution)/shard_map/psum | solution.py:38
  471.5 6.8 %all-to-all-start.12 = ((f32[128,1,256]{2,1,0:T(1,128)}), f32[128,1,256]{2,1,0:T(1,128)S(1)}, u32[]{:S(2)}, u32[]{:S(2)}) async-start(f32[128,1,256]{2,1,0:T(1,128)} %reshape.638), calls=%async_computation.12 | async-start | bytes 262144 | tf_op jit(solution)/shard_map/all_to_all | solution.py:123
  479.8 6.4 all-to-all-done.12
  486.2 7.4 %all-to-all-start.13 = ((f32[128,1,256]{2,1,0:T(1,128)}), f32[128,1,256]{2,1,0:T(1,128)}, u32[]{:S(2)}, u32[]{:S(2)}) async-start(f32[128,1,256]{2,1,0:T(1,128)} %reshape.640), calls=%async_computation.13 | async-start | bytes 262144 | tf_op jit(solution)/shard_map/all_to_all | solution.py:124
  522.6 7.8 %all-to-all-start.14 = ((f32[128,1,256]{2,1,0:T(1,128)}), f32[128,1,256]{2,1,0:T(1,128)}, u32[]{:S(2)}, u32[]{:S(2)}) async-start(f32[128,1,256]{2,1,0:T(1,128)} %reshape.642), calls=%async_computation.14 | async-start | bytes 262144 | tf_op jit(solution)/shard_map/all_to_all | solution.py:135
  532.6 5.4 all-to-all-done.14
  537.9 6.5 %all-to-all-start.15 = ((f32[128,1,256]{2,1,0:T(1,128)}), f32[128,1,256]{2,1,0:T(1,128)S(1)}, u32[]{:S(2)}, u32[]{:S(2)}) async-start(f32[128,1,256]{2,1,0:T(1,128)} %reshape.644), calls=%async_computation.15 | async-start | bytes 262144 | tf_op jit(solution)/shard_map/all_to_all | solution.py:136
  547.5 4.9 all-to-all-done.15
  555.2 4.4 psum.310
  559.6 7.7 %psum.311 = f32[]{:T(128)} all-reduce(f32[]{:T(128)} %psum.310), channel_id=1, replica_groups=mesh['pa_0'=2,'pa_1'=4,'pb_0'=2,'pb_1'=4,'pb_2'=2] {'pa_1'}, use_global_device_ids=true, to_apply=%region_38.39 | all-reduce | flops 1 | bytes 8 | tf_op jit(solution)/shard_map/psum | solution.py:38
  567.3 5.9 psum.312
  573.2 7.7 %psum.313 = f32[]{:T(128)} all-reduce(f32[]{:T(128)} %psum.312), channel_id=1, replica_groups=mesh['pa_0'=2,'pa_1'=4,'pb_0'=2,'pb_1'=4,'pb_2'=2] {'pb_1'}, use_global_device_ids=true, to_apply=%region_40.41 | all-reduce | flops 1 | bytes 8 | tf_op jit(solution)/shard_map/psum | solution.py:38
  580.9 9.7 %psum.314 = f32[]{:T(128)} all-reduce(f32[]{:T(128)} %psum.313), channel_id=1, replica_groups=mesh['pa_0'=2,'pa_1'=4,'pb_0'=2,'pb_1'=4,'pb_2'=2] {'pb_2'}, use_global_device_ids=true, to_apply=%region_41.42 | all-reduce | flops 1 | bytes 8 | tf_op jit(solution)/shard_map/psum | solution.py:38
  597.5 4.4 psum.315
  601.9 9.5 %psum.316 = f32[]{:T(128)} all-reduce(f32[]{:T(128)} %psum.315), channel_id=1, replica_groups=mesh['pa_0'=2,'pa_1'=4,'pb_0'=2,'pb_1'=4,'pb_2'=2] {'pa_1'}, use_global_device_ids=true, to_apply=%region_44.45 | all-reduce | flops 1 | bytes 8 | tf_op jit(solution)/shard_map/psum | solution.py:38
  611.5 5.9 psum.317
  617.4 9.0 %psum.318 = f32[]{:T(128)} all-reduce(f32[]{:T(128)} %psum.317), channel_id=1, replica_groups=mesh['pa_0'=2,'pa_1'=4,'pb_0'=2,'pb_1'=4,'pb_2'=2] {'pb_1'}, use_global_device_ids=true, to_apply=%region_46.47 | all-reduce | flops 1 | bytes 8 | tf_op jit(solution)/shard_map/psum | solution.py:38
  626.4 13.2 %psum.319 = f32[]{:T(128)} all-reduce(f32[]{:T(128)} %psum.318), channel_id=1, replica_groups=mesh['pa_0'=2,'pa_1'=4,'pb_0'=2,'pb_1'=4,'pb_2'=2] {'pb_2'}, use_global_device_ids=true, to_apply=%region_47.48 | all-reduce | flops 1 | bytes 8 | tf_op jit(solution)/shard_map/psum | solution.py:38
  (297 shorter events, 181.3 us)
Async XLA Ops:
  2.1 90.8 %collective-permute-start.4 = (f32[128,16,1]{0,2,1:T(1,128)}, f32[128,16,1]{0,2,1:T(1,128)S(1)}, u32[]{:S(2)}, u32[]{:S(2)}) collective-permute-start(f32[128,16,1]{0,2,1:T(1,128)} %slice.196), channel_id=1, source_target_pairs={{0,1},{1,2},{2,3},{3,4},{4,5},{5,6},{6,7},{7,8},{8,9},{9,10},{10,1... | collective-permute-start | bytes 24584 | tf_op jit(solution)/shard_map/ppermute | solution.py:45
  4.5 89.5 %collective-permute-start.1 = (f32[128,1,16]{0,2,1:T(8,128)S(1)}, f32[128,1,16]{0,2,1:T(8,128)S(1)}, u32[]{:S(2)}, u32[]{:S(2)}) collective-permute-start(f32[128,1,16]{0,2,1:T(8,128)S(1)} %slice.190), channel_id=1, source_target_pairs={{0,16},{16,32},{32,48},{48,64},{64,80},{80,96},{96,112},{112,0},{1... | collective-permute-start | bytes 24584 | tf_op jit(solution)/shard_map/ppermute | solution.py:45
  8.8 9.6 %copy-start.7 = (f32[128,16,16]{0,2,1:T(8,128)S(1)}, f32[128,16,16]{0,2,1:T(8,128)}, u32[]{:S(2)}) copy-start(f32[128,16,16]{0,2,1:T(8,128)} %param.4) | copy-start | bytes 393220
  8.8 17.5 %all-to-all-start = ((f32[128,1,256]{2,1,0:T(1,128)}), f32[128,1,256]{2,1,0:T(1,128)S(1)}, u32[]{:S(2)}, u32[]{:S(2)}) async-start(f32[128,1,256]{2,1,0:T(1,128)} %reshape.614), calls=%async_computation | async-start | bytes 262144 | tf_op jit(solution)/shard_map/all_to_all | solution.py:123
  19.0 0.9 copy-start.2
  19.0 0.9 copy-start.1
  26.3 14.3 %all-to-all-start.1 = ((f32[128,1,256]{2,1,0:T(1,128)}), f32[128,1,256]{2,1,0:T(1,128)S(1)}, u32[]{:S(2)}, u32[]{:S(2)}) async-start(f32[128,1,256]{2,1,0:T(1,128)} %reshape.616), calls=%async_computation.1 | async-start | bytes 262144 | tf_op jit(solution)/shard_map/all_to_all | solution.py:124
  45.7 1.6 copy-start.16
  45.7 1.6 copy-start.18
  59.9 14.2 %all-to-all-start.2 = ((f32[128,1,256]{2,1,0:T(1,128)}), f32[128,1,256]{2,1,0:T(1,128)S(1)}, u32[]{:S(2)}, u32[]{:S(2)}) async-start(f32[128,1,256]{2,1,0:T(1,128)} %reshape.618), calls=%async_computation.2 | async-start | bytes 262144 | tf_op jit(solution)/shard_map/all_to_all | solution.py:135
  74.1 14.1 %all-to-all-start.3 = ((f32[128,1,256]{2,1,0:T(1,128)}), f32[128,1,256]{2,1,0:T(1,128)S(1)}, u32[]{:S(2)}, u32[]{:S(2)}) async-start(f32[128,1,256]{2,1,0:T(1,128)} %reshape.620), calls=%async_computation.3 | async-start | bytes 262144 | tf_op jit(solution)/shard_map/all_to_all | solution.py:136
  90.6 3.4 collective-permute-start.3
  91.1 2.9 collective-permute-start.5
  92.4 2.5 collective-permute-start.2
  92.9 2.6 copy-start
  92.9 2.6 collective-permute-start
  139.5 15.2 %all-to-all-start.4 = ((f32[128,1,256]{2,1,0:T(1,128)}), f32[128,1,256]{2,1,0:T(1,128)S(1)}, u32[]{:S(2)}, u32[]{:S(2)}) async-start(f32[128,1,256]{2,1,0:T(1,128)} %reshape.622), calls=%async_computation.4 | async-start | bytes 262144 | tf_op jit(solution)/shard_map/all_to_all | solution.py:123
  154.6 14.3 %all-to-all-start.5 = ((f32[128,1,256]{2,1,0:T(1,128)}), f32[128,1,256]{2,1,0:T(1,128)S(1)}, u32[]{:S(2)}, u32[]{:S(2)}) async-start(f32[128,1,256]{2,1,0:T(1,128)} %reshape.624), calls=%async_computation.5 | async-start | bytes 262144 | tf_op jit(solution)/shard_map/all_to_all | solution.py:124
  174.1 1.6 copy-start.17
  174.1 1.6 copy-start.19
  188.3 14.2 %all-to-all-start.6 = ((f32[128,1,256]{2,1,0:T(1,128)}), f32[128,1,256]{2,1,0:T(1,128)S(1)}, u32[]{:S(2)}, u32[]{:S(2)}) async-start(f32[128,1,256]{2,1,0:T(1,128)} %reshape.626), calls=%async_computation.6 | async-start | bytes 262144 | tf_op jit(solution)/shard_map/all_to_all | solution.py:135
  202.5 14.1 %all-to-all-start.7 = ((f32[128,1,256]{2,1,0:T(1,128)}), f32[128,1,256]{2,1,0:T(1,128)S(1)}, u32[]{:S(2)}, u32[]{:S(2)}) async-start(f32[128,1,256]{2,1,0:T(1,128)} %reshape.628), calls=%async_computation.7 | async-start | bytes 262144 | tf_op jit(solution)/shard_map/all_to_all | solution.py:136
  256.5 3.4 collective-permute-start.8
  256.9 3.0 collective-permute-start.9
  258.3 2.5 collective-permute-start.7
  258.3 2.5 collective-permute-start.6
  301.7 84.5 %copy-start.3 = (f32[128,16,16]{0,2,1:T(8,128)}, f32[128,16,16]{0,2,1:T(8,128)S(1)}, u32[]{:S(2)}) copy-start(f32[128,16,16]{0,2,1:T(8,128)S(1)} %multiply_subtract_fusion.2) | copy-start | bytes 393220
  304.3 14.7 %all-to-all-start.8 = ((f32[128,1,256]{2,1,0:T(1,128)}), f32[128,1,256]{2,1,0:T(1,128)S(1)}, u32[]{:S(2)}, u32[]{:S(2)}) async-start(f32[128,1,256]{2,1,0:T(1,128)} %reshape.630), calls=%async_computation.8 | async-start | bytes 262144 | tf_op jit(solution)/shard_map/all_to_all | solution.py:123
  319.1 14.9 %all-to-all-start.9 = ((f32[128,1,256]{2,1,0:T(1,128)}), f32[128,1,256]{2,1,0:T(1,128)}, u32[]{:S(2)}, u32[]{:S(2)}) async-start(f32[128,1,256]{2,1,0:T(1,128)} %reshape.632), calls=%async_computation.9 | async-start | bytes 262144 | tf_op jit(solution)/shard_map/all_to_all | solution.py:124
  336.8 0.9 copy-start.14
  349.3 3.1 copy-start.8
  355.2 6.8 %copy-start.9 = (f32[128,256]{0,1:T(8,128)S(1)}, f32[128,256]{0,1:T(8,128)}, u32[]{:S(2)}) copy-start(f32[128,256]{0,1:T(8,128)} %copy-done.8) | copy-start | bytes 393220
  355.2 6.8 %copy-start.12 = (f32[128,256]{1,0:T(8,128)S(1)}, f32[128,256]{1,0:T(8,128)}, u32[]{:S(2)}) copy-start(f32[128,256]{1,0:T(8,128)} %fusion.196) | copy-start | bytes 393220
  355.2 14.7 %all-to-all-start.10 = ((f32[128,1,256]{2,1,0:T(1,128)}), f32[128,1,256]{2,1,0:T(1,128)S(1)}, u32[]{:S(2)}, u32[]{:S(2)}) async-start(f32[128,1,256]{2,1,0:T(1,128)} %reshape.634), calls=%async_computation.10 | async-start | bytes 262144 | tf_op jit(solution)/shard_map/all_to_all | solution.py:135
  369.9 14.1 %all-to-all-start.11 = ((f32[128,1,256]{2,1,0:T(1,128)}), f32[128,1,256]{2,1,0:T(1,128)S(1)}, u32[]{:S(2)}, u32[]{:S(2)}) async-start(f32[128,1,256]{2,1,0:T(1,128)} %reshape.636), calls=%async_computation.11 | async-start | bytes 262144 | tf_op jit(solution)/shard_map/all_to_all | solution.py:136
  423.7 3.4 collective-permute-start.12
  424.1 3.0 collective-permute-start.13
  425.5 2.5 collective-permute-start.11
  425.5 2.5 collective-permute-start.10
  428.0 40.8 %copy-start.4 = (f32[128,16,16]{0,2,1:T(8,128)S(1)}, f32[128,16,16]{0,2,1:T(8,128)}, u32[]{:S(2)}) copy-start(f32[128,16,16]{0,2,1:T(8,128)} %copy-done.3) | copy-start | bytes 393220
  471.5 14.7 %all-to-all-start.12 = ((f32[128,1,256]{2,1,0:T(1,128)}), f32[128,1,256]{2,1,0:T(1,128)S(1)}, u32[]{:S(2)}, u32[]{:S(2)}) async-start(f32[128,1,256]{2,1,0:T(1,128)} %reshape.638), calls=%async_computation.12 | async-start | bytes 262144 | tf_op jit(solution)/shard_map/all_to_all | solution.py:123
  486.2 14.9 %all-to-all-start.13 = ((f32[128,1,256]{2,1,0:T(1,128)}), f32[128,1,256]{2,1,0:T(1,128)}, u32[]{:S(2)}, u32[]{:S(2)}) async-start(f32[128,1,256]{2,1,0:T(1,128)} %reshape.640), calls=%async_computation.13 | async-start | bytes 262144 | tf_op jit(solution)/shard_map/all_to_all | solution.py:124
  495.7 1.2 copy-start.5
  504.0 0.9 copy-start.15
  504.9 0.9 copy-start.6
  516.9 3.0 copy-start.10
  522.5 7.8 %copy-start.11 = (f32[128,256]{0,1:T(8,128)S(1)}, f32[128,256]{0,1:T(8,128)}, u32[]{:S(2)}) copy-start(f32[128,256]{0,1:T(8,128)} %copy-done.10) | copy-start | bytes 393220
  522.6 7.8 %copy-start.13 = (f32[128,256]{1,0:T(8,128)S(1)}, f32[128,256]{1,0:T(8,128)}, u32[]{:S(2)}) copy-start(f32[128,256]{1,0:T(8,128)} %fusion.184) | copy-start | bytes 393220
  522.6 15.4 %all-to-all-start.14 = ((f32[128,1,256]{2,1,0:T(1,128)}), f32[128,1,256]{2,1,0:T(1,128)}, u32[]{:S(2)}, u32[]{:S(2)}) async-start(f32[128,1,256]{2,1,0:T(1,128)} %reshape.642), calls=%async_computation.14 | async-start | bytes 262144 | tf_op jit(solution)/shard_map/all_to_all | solution.py:135
  537.9 14.4 %all-to-all-start.15 = ((f32[128,1,256]{2,1,0:T(1,128)}), f32[128,1,256]{2,1,0:T(1,128)S(1)}, u32[]{:S(2)}, u32[]{:S(2)}) async-start(f32[128,1,256]{2,1,0:T(1,128)} %reshape.644), calls=%async_computation.15 | async-start | bytes 262144 | tf_op jit(solution)/shard_map/all_to_all | solution.py:136
  592.1 3.4 collective-permute-start.15
  592.2 3.3 collective-permute-start.14
  593.7 3.1 collective-permute-start.16
  594.6 2.2 collective-permute-start.17
where the time goes:
time: 648 us; the launch traced here: 642 us
  blocking collectives  265 us (41%)
  starting transfers between devices  126 us (19%)
  waiting for transfers between devices  90.7 us (14%)
  matrix products  77.7 us (12%)
  local copies, waits for them, and re-layouts  45.4 us (7%)
  other arithmetic  25 us (4%)
  between operations  11.7 us (2%)
    psum x35, blocking collectives, by_axis(): x = lax.psum(x, axis)  265 us
    dot_general x64, matrix products, apply_along(): jnp.tensordot(matrix, values, axes=([1], [target_dim]), precision=lax.Pre...  68.4 us
    all_to_all x4, starting transfers between devices, precondition(): lax.all_to_all(stacked_real, PA_PB, split_axis=0, concat_axis=0, tiled=True)  30.4 us
    all_to_all x4, starting transfers between devices, precondition(): lax.all_to_all(stacked_imag, PA_PB, split_axis=0, concat_axis=0, tiled=True)  27.8 us
    all_to_all x4, starting transfers between devices, precondition(): lax.all_to_all(from_slab(real_part), PA_PB, split_axis=0, concat_axis=0,...  27.1 us
    all_to_all x4, starting transfers between devices, precondition(): lax.all_to_all(from_slab(imag_part), PA_PB, split_axis=0, concat_axis=0,...  25 us
    unnamed x72, local copies, waits for them, and re-layouts  23.5 us
    all_to_all x4, waiting for transfers between devices, precondition(): lax.all_to_all(stacked_real, PA_PB, split_axis=0, concat_axis=0, tiled=True)  23.2 us
  transfers between devices with their start and end apart: 34, of which 21 were waited for; matrix products, arithmetic and copies ran while one was open for 10% of the time, Pallas kernels for 0%

commit v1 on v0

--- a/solution.py
+++ b/solution.py
@@ -35,7 +35,7 @@
 
 def by_axis(x, axes):
     for axis in axes:
-        x = lax.psum(x, axis)
+        x = jnp.sum(lax.all_gather(x, axis), axis=0)
     return x
 
 

time: 648 us -> 711 us (1.097)
  local copies, waits for them, and re-layouts: 45.4 us -> 103 us
  other arithmetic: 25 us -> 48.3 us
  blocking collectives: 265 us -> 245 us
    psum x35 -> x0, blocking collectives: 265 us -> none  [by_axis(): x = lax.psum(x, axis)]
    unnamed x0 -> x35, blocking collectives: none -> 245 us
    unnamed x72 -> x167, local copies, waits for them, and re-layouts: 23.5 us -> 82.4 us
    reduce_sum x0 -> x40, other arithmetic: none -> 24.2 us  [by_axis(): x = jnp.sum(lax.all_gather(x, axis), axis=0)]
  transfers between devices with their start and end apart: 34 -> 34, of which waited for: 21 -> 20; matrix products, arithmetic and copies ran while one was open for 10% -> 9% of each run, Pallas kernels for 0% -> 0%
where the time goes in v1:
time: 711 us; the launch traced here: 702 us
  blocking collectives  245 us (34%)
  starting transfers between devices  130 us (18%)
  local copies, waits for them, and re-layouts  103 us (14%)
  waiting for transfers between devices  86.2 us (12%)
  matrix products  77.6 us (11%)
  other arithmetic  48.3 us (7%)
  between operations  12 us (2%)
    unnamed x35, blocking collectives  245 us
    unnamed x167, local copies, waits for them, and re-layouts  82.4 us
    dot_general x64, matrix products, apply_along(): jnp.tensordot(matrix, values, axes=([1], [target_dim]), precision=lax.Pre...  68.4 us
    all_to_all x4, starting transfers between devices, precondition(): lax.all_to_all(stacked_imag, PA_PB, split_axis=0, concat_axis=0, tiled=True)  32.1 us
    all_to_all x4, starting transfers between devices, precondition(): lax.all_to_all(stacked_real, PA_PB, split_axis=0, concat_axis=0, tiled=True)  30.3 us
    all_to_all x4, starting transfers between devices, precondition(): lax.all_to_all(from_slab(imag_part), PA_PB, split_axis=0, concat_axis=0,...  26.9 us
    all_to_all x4, starting transfers between devices, precondition(): lax.all_to_all(from_slab(real_part), PA_PB, split_axis=0, concat_axis=0,...  25 us
    reduce_sum x40, other arithmetic, by_axis(): x = jnp.sum(lax.all_gather(x, axis), axis=0)  24.2 us
  transfers between devices with their start and end apart: 34, of which 20 were waited for; matrix products, arithmetic and copies ran while one was open for 9% of the time, Pallas kernels for 0%

profile of v1, /device:TPU:11, one launch (start us, length us, event | category | flops | bytes accessed | tf_op | source)
XLA Modules:
  0.0 702.2 jit_solution(12348081916679450091)
XLA Ops:
  3.6 10.7 %all-to-all-start.1 = ((f32[128,1,256]{2,1,0:T(1,128)}), f32[128,1,256]{2,1,0:T(1,128)S(1)}, u32[]{:S(2)}, u32[]{:S(2)}) async-start(f32[128,1,256]{2,1,0:T(1,128)} %reshape.816), calls=%async_computation.1 | async-start | bytes 262144 | tf_op jit(solution)/shard_map/all_to_all | solution.py:124
  22.8 9.3 %all-to-all-start = ((f32[128,1,256]{2,1,0:T(1,128)}), f32[128,1,256]{2,1,0:T(1,128)S(1)}, u32[]{:S(2)}, u32[]{:S(2)}) async-start(f32[128,1,256]{2,1,0:T(1,128)} %reshape.814), calls=%async_computation | async-start | bytes 262144 | tf_op jit(solution)/shard_map/all_to_all | solution.py:123
  35.0 4.8 all-to-all-done
  59.1 6.3 all-to-all-start.3
  67.6 5.7 all-to-all-done.3
  73.4 6.2 all-to-all-start.2
  81.7 5.8 all-to-all-done.2
  106.9 8.2 %all-reduce.49 = (f32[4]{0:T(128)S(1)}, f32[4]{0:T(128)S(1)}) all-reduce(f32[4]{0:T(128)S(1)} %dynamic-update-slice.1, f32[4]{0:T(128)S(1)} %dynamic-update-slice.6), channel_id=1, replica_groups=mesh['pa_0'=2,'pa_1'=4,'pb_0'=2,'pb_1'=4,'pb_2'=2] {'pa_1'}, use_global_device_ids=true, to_apply=%add.9 | all-reduce | flops 8 | bytes 64
  119.6 5.3 all-reduce.51
  129.6 8.7 %all-reduce.48 = (f32[4]{0:T(128)S(1)}, f32[4]{0:T(128)S(1)}) all-reduce(f32[4]{0:T(128)S(1)} %dynamic-update-slice.3, f32[4]{0:T(128)S(1)} %dynamic-update-slice.8), channel_id=1, replica_groups=mesh['pa_0'=2,'pa_1'=4,'pb_0'=2,'pb_1'=4,'pb_2'=2] {'pb_1'}, use_global_device_ids=true, to_apply=%add.11 | all-reduce | flops 8 | bytes 64
  142.4 11.9 %all-reduce.50 = (f32[2]{0:T(128)S(1)}, f32[2]{0:T(128)S(1)}) all-reduce(f32[2]{0:T(128)S(1)} %dynamic-update-slice.4, f32[2]{0:T(128)S(1)} %dynamic-update-slice.9), channel_id=1, replica_groups=mesh['pa_0'=2,'pa_1'=4,'pb_0'=2,'pb_1'=4,'pb_2'=2] {'pb_2'}, use_global_device_ids=true, to_apply=%add.12 | all-reduce | flops 4 | bytes 32
  159.1 7.6 %all-to-all-start.5 = ((f32[128,1,256]{2,1,0:T(1,128)}), f32[128,1,256]{2,1,0:T(1,128)S(1)}, u32[]{:S(2)}, u32[]{:S(2)}) async-start(f32[128,1,256]{2,1,0:T(1,128)} %reshape.824), calls=%async_computation.5 | async-start | bytes 262144 | tf_op jit(solution)/shard_map/all_to_all | solution.py:124
  168.7 5.9 all-to-all-done.5
  174.6 6.2 all-to-all-start.4
  183.3 5.4 all-to-all-done.4
  208.0 6.2 all-to-all-start.7
  216.4 5.7 all-to-all-done.7
  222.1 6.2 all-to-all-start.6
  230.5 5.8 all-to-all-done.6
  240.4 3.8 all-reduce.18
  246.2 7.1 %all-reduce.19 = f32[4]{0:T(128)S(1)} all-reduce(f32[4]{0:T(128)S(1)} %dynamic-update-slice.11), channel_id=1, replica_groups=mesh['pa_0'=2,'pa_1'=4,'pb_0'=2,'pb_1'=4,'pb_2'=2] {'pa_1'}, use_global_device_ids=true, to_apply=%add.19 | all-reduce | flops 4 | bytes 32
  255.1 5.3 all-reduce.20
  262.4 7.1 %all-reduce.21 = f32[4]{0:T(128)S(1)} all-reduce(f32[4]{0:T(128)S(1)} %dynamic-update-slice.13), channel_id=1, replica_groups=mesh['pa_0'=2,'pa_1'=4,'pb_0'=2,'pb_1'=4,'pb_2'=2] {'pb_1'}, use_global_device_ids=true, to_apply=%add.21 | all-reduce | flops 4 | bytes 32
  271.6 9.1 %all-reduce.22 = f32[2]{0:T(128)S(1)} all-reduce(f32[2]{0:T(128)S(1)} %dynamic-update-slice.14), channel_id=1, replica_groups=mesh['pa_0'=2,'pa_1'=4,'pb_0'=2,'pb_1'=4,'pb_2'=2] {'pb_2'}, use_global_device_ids=true, to_apply=%add.22 | all-reduce | flops 2 | bytes 16
  295.4 7.5 %all-reduce.24 = f32[4]{0:T(128)S(1)} all-reduce(f32[4]{0:T(128)S(1)} %dynamic-update-slice.16), channel_id=1, replica_groups=mesh['pa_0'=2,'pa_1'=4,'pb_0'=2,'pb_1'=4,'pb_2'=2] {'pa_1'}, use_global_device_ids=true, to_apply=%add.24 | all-reduce | flops 4 | bytes 32
  304.8 5.3 all-reduce.25
  312.1 7.7 %all-reduce.26 = f32[4]{0:T(128)S(1)} all-reduce(f32[4]{0:T(128)S(1)} %dynamic-update-slice.18), channel_id=1, replica_groups=mesh['pa_0'=2,'pa_1'=4,'pb_0'=2,'pb_1'=4,'pb_2'=2] {'pb_1'}, use_global_device_ids=true, to_apply=%add.26 | all-reduce | flops 4 | bytes 32
  321.9 12.5 %all-reduce.27 = f32[2]{0:T(128)S(1)} all-reduce(f32[2]{0:T(128)S(1)} %dynamic-update-slice.19), channel_id=1, replica_groups=mesh['pa_0'=2,'pa_1'=4,'pb_0'=2,'pb_1'=4,'pb_2'=2] {'pb_2'}, use_global_device_ids=true, to_apply=%add.27 | all-reduce | flops 2 | bytes 16
  338.4 6.9 all-to-all-start.9
  347.4 5.9 all-to-all-done.9
  353.3 7.4 %all-to-all-start.8 = ((f32[128,1,256]{2,1,0:T(1,128)}), f32[128,1,256]{2,1,0:T(1,128)}, u32[]{:S(2)}, u32[]{:S(2)}) async-start(f32[128,1,256]{2,1,0:T(1,128)} %reshape.830), calls=%async_computation.8 | async-start | bytes 262144 | tf_op jit(solution)/shard_map/all_to_all | solution.py:123
  363.8 4.3 all-to-all-done.8
  389.5 6.7 all-to-all-start.11
  398.4 5.8 all-to-all-done.11
  404.2 6.2 all-to-all-start.10
  412.5 5.8 all-to-all-done.10
  422.4 3.8 all-reduce.28
  428.2 7.1 %all-reduce.29 = f32[4]{0:T(128)S(1)} all-reduce(f32[4]{0:T(128)S(1)} %dynamic-update-slice.21), channel_id=1, replica_groups=mesh['pa_0'=2,'pa_1'=4,'pb_0'=2,'pb_1'=4,'pb_2'=2] {'pa_1'}, use_global_device_ids=true, to_apply=%add.29 | all-reduce | flops 4 | bytes 32
  437.2 5.3 all-reduce.30
  444.5 7.1 %all-reduce.31 = f32[4]{0:T(128)S(1)} all-reduce(f32[4]{0:T(128)S(1)} %dynamic-update-slice.23), channel_id=1, replica_groups=mesh['pa_0'=2,'pa_1'=4,'pb_0'=2,'pb_1'=4,'pb_2'=2] {'pb_1'}, use_global_device_ids=true, to_apply=%add.31 | all-reduce | flops 4 | bytes 32
  453.6 9.1 %all-reduce.32 = f32[2]{0:T(128)S(1)} all-reduce(f32[2]{0:T(128)S(1)} %dynamic-update-slice.24), channel_id=1, replica_groups=mesh['pa_0'=2,'pa_1'=4,'pb_0'=2,'pb_1'=4,'pb_2'=2] {'pb_2'}, use_global_device_ids=true, to_apply=%add.32 | all-reduce | flops 2 | bytes 16
  471.6 3.8 all-reduce.33
  477.4 7.5 %all-reduce.34 = f32[4]{0:T(128)S(1)} all-reduce(f32[4]{0:T(128)S(1)} %dynamic-update-slice.26), channel_id=1, replica_groups=mesh['pa_0'=2,'pa_1'=4,'pb_0'=2,'pb_1'=4,'pb_2'=2] {'pa_1'}, use_global_device_ids=true, to_apply=%add.34 | all-reduce | flops 4 | bytes 32
  486.8 5.3 all-reduce.35
  494.1 7.7 %all-reduce.36 = f32[4]{0:T(128)S(1)} all-reduce(f32[4]{0:T(128)S(1)} %dynamic-update-slice.28), channel_id=1, replica_groups=mesh['pa_0'=2,'pa_1'=4,'pb_0'=2,'pb_1'=4,'pb_2'=2] {'pb_1'}, use_global_device_ids=true, to_apply=%add.36 | all-reduce | flops 4 | bytes 32
  503.9 12.5 %all-reduce.37 = f32[2]{0:T(128)S(1)} all-reduce(f32[2]{0:T(128)S(1)} %dynamic-update-slice.29), channel_id=1, replica_groups=mesh['pa_0'=2,'pa_1'=4,'pb_0'=2,'pb_1'=4,'pb_2'=2] {'pb_2'}, use_global_device_ids=true, to_apply=%add.37 | all-reduce | flops 2 | bytes 16
  520.4 6.9 all-to-all-start.13
  529.4 5.9 all-to-all-done.13
  535.3 7.4 %all-to-all-start.12 = ((f32[128,1,256]{2,1,0:T(1,128)}), f32[128,1,256]{2,1,0:T(1,128)}, u32[]{:S(2)}, u32[]{:S(2)}) async-start(f32[128,1,256]{2,1,0:T(1,128)} %reshape.838), calls=%async_computation.12 | async-start | bytes 262144 | tf_op jit(solution)/shard_map/all_to_all | solution.py:123
  545.9 4.3 all-to-all-done.12
  571.3 7.8 %all-to-all-start.15 = ((f32[128,1,256]{2,1,0:T(1,128)}), f32[128,1,256]{2,1,0:T(1,128)}, u32[]{:S(2)}, u32[]{:S(2)}) async-start(f32[128,1,256]{2,1,0:T(1,128)} %reshape.844), calls=%async_computation.15 | async-start | bytes 262144 | tf_op jit(solution)/shard_map/all_to_all | solution.py:136
  581.3 5.4 all-to-all-done.15
  586.7 6.5 all-to-all-start.14
  596.2 4.9 all-to-all-done.14
  605.3 3.8 all-reduce.38
  611.0 7.1 %all-reduce.39 = f32[4]{0:T(128)S(1)} all-reduce(f32[4]{0:T(128)S(1)} %dynamic-update-slice.31), channel_id=1, replica_groups=mesh['pa_0'=2,'pa_1'=4,'pb_0'=2,'pb_1'=4,'pb_2'=2] {'pa_1'}, use_global_device_ids=true, to_apply=%add.39 | all-reduce | flops 4 | bytes 32
  620.0 5.3 all-reduce.40
  627.3 7.1 %all-reduce.41 = f32[4]{0:T(128)S(1)} all-reduce(f32[4]{0:T(128)S(1)} %dynamic-update-slice.33), channel_id=1, replica_groups=mesh['pa_0'=2,'pa_1'=4,'pb_0'=2,'pb_1'=4,'pb_2'=2] {'pb_1'}, use_global_device_ids=true, to_apply=%add.41 | all-reduce | flops 4 | bytes 32
  636.5 9.1 %all-reduce.42 = f32[2]{0:T(128)S(1)} all-reduce(f32[2]{0:T(128)S(1)} %dynamic-update-slice.34), channel_id=1, replica_groups=mesh['pa_0'=2,'pa_1'=4,'pb_0'=2,'pb_1'=4,'pb_2'=2] {'pb_2'}, use_global_device_ids=true, to_apply=%add.42 | all-reduce | flops 2 | bytes 16
  654.5 3.8 all-reduce.43
  660.2 7.5 %all-reduce.44 = f32[4]{0:T(128)S(1)} all-reduce(f32[4]{0:T(128)S(1)} %dynamic-update-slice.36), channel_id=1, replica_groups=mesh['pa_0'=2,'pa_1'=4,'pb_0'=2,'pb_1'=4,'pb_2'=2] {'pa_1'}, use_global_device_ids=true, to_apply=%add.44 | all-reduce | flops 4 | bytes 32
  669.7 5.3 all-reduce.45
  677.0 7.7 %all-reduce.46 = f32[4]{0:T(128)S(1)} all-reduce(f32[4]{0:T(128)S(1)} %dynamic-update-slice.38), channel_id=1, replica_groups=mesh['pa_0'=2,'pa_1'=4,'pb_0'=2,'pb_1'=4,'pb_2'=2] {'pb_1'}, use_global_device_ids=true, to_apply=%add.46 | all-reduce | flops 4 | bytes 32
  686.8 12.5 %all-reduce.47 = f32[2]{0:T(128)S(1)} all-reduce(f32[2]{0:T(128)S(1)} %dynamic-update-slice.39), channel_id=1, replica_groups=mesh['pa_0'=2,'pa_1'=4,'pb_0'=2,'pb_1'=4,'pb_2'=2] {'pb_2'}, use_global_device_ids=true, to_apply=%add.47 | all-reduce | flops 2 | bytes 16
  (432 shorter events, 257.2 us)
Async XLA Ops:
  2.6 15.4 %copy-start.7 = (f32[128,16,16]{0,2,1:T(8,128)S(1)}, f32[128,16,16]{0,2,1:T(8,128)}, u32[]{:S(2)}) copy-start(f32[128,16,16]{0,2,1:T(8,128)} %param.4) | copy-start | bytes 393220
  3.6 10.7 %copy-start.2 = (f32[128,16,16]{0,2,1:T(8,128)S(1)}, f32[128,16,16]{0,2,1:T(8,128)}, u32[]{:S(2)}) copy-start(f32[128,16,16]{0,2,1:T(8,128)} %param.6) | copy-start | bytes 393220
  3.6 12.5 %copy-start = (f32[128,16,16]{0,2,1:T(8,128)S(1)}, f32[128,16,16]{0,2,1:T(8,128)}, u32[]{:S(2)}) copy-start(f32[128,16,16]{0,2,1:T(8,128)} %param.7) | copy-start | bytes 393220
  3.6 19.1 %all-to-all-start.1 = ((f32[128,1,256]{2,1,0:T(1,128)}), f32[128,1,256]{2,1,0:T(1,128)S(1)}, u32[]{:S(2)}, u32[]{:S(2)}) async-start(f32[128,1,256]{2,1,0:T(1,128)} %reshape.816), calls=%async_computation.1 | async-start | bytes 262144 | tf_op jit(solution)/shard_map/all_to_all | solution.py:124
  14.9 77.3 %collective-permute-start.1 = (f32[128,1,16]{0,2,1:T(8,128)}, f32[128,1,16]{0,2,1:T(8,128)S(1)}, u32[]{:S(2)}, u32[]{:S(2)}) collective-permute-start(f32[128,1,16]{0,2,1:T(8,128)} %slice.190), channel_id=1, source_target_pairs={{0,16},{16,32},{32,48},{48,64},{64,80},{80,96},{96,112},{112,0},{1... | collective-permute-start | bytes 24584 | tf_op jit(solution)/shard_map/ppermute | solution.py:45
  16.2 77.0 %collective-permute-start.4 = (f32[128,16,1]{0,2,1:T(1,128)S(1)}, f32[128,16,1]{0,2,1:T(1,128)S(1)}, u32[]{:S(2)}, u32[]{:S(2)}) collective-permute-start(f32[128,16,1]{0,2,1:T(1,128)S(1)} %slice.196), channel_id=1, source_target_pairs={{0,1},{1,2},{2,3},{3,4},{4,5},{5,6},{6,7},{7,8},{8,9},{9,10},{10,1... | collective-permute-start | bytes 24584 | tf_op jit(solution)/shard_map/ppermute | solution.py:45
  19.7 1.1 copy-start.1
  20.9 0.7 copy-start.20
  22.8 17.1 %all-to-all-start = ((f32[128,1,256]{2,1,0:T(1,128)}), f32[128,1,256]{2,1,0:T(1,128)S(1)}, u32[]{:S(2)}, u32[]{:S(2)}) async-start(f32[128,1,256]{2,1,0:T(1,128)} %reshape.814), calls=%async_computation | async-start | bytes 262144 | tf_op jit(solution)/shard_map/all_to_all | solution.py:123
  44.9 1.6 copy-start.21
  44.9 1.6 copy-start.23
  59.1 14.2 %all-to-all-start.3 = ((f32[128,1,256]{2,1,0:T(1,128)}), f32[128,1,256]{2,1,0:T(1,128)S(1)}, u32[]{:S(2)}, u32[]{:S(2)}) async-start(f32[128,1,256]{2,1,0:T(1,128)} %reshape.820), calls=%async_computation.3 | async-start | bytes 262144 | tf_op jit(solution)/shard_map/all_to_all | solution.py:136
  73.4 14.1 %all-to-all-start.2 = ((f32[128,1,256]{2,1,0:T(1,128)}), f32[128,1,256]{2,1,0:T(1,128)S(1)}, u32[]{:S(2)}, u32[]{:S(2)}) async-start(f32[128,1,256]{2,1,0:T(1,128)} %reshape.818), calls=%async_computation.2 | async-start | bytes 262144 | tf_op jit(solution)/shard_map/all_to_all | solution.py:135
  89.8 3.4 collective-permute-start
  91.0 2.5 collective-permute-start.2
  91.3 3.1 collective-permute-start.3
  92.3 2.1 collective-permute-start.5
  96.6 1.4 copy-start.19
  105.0 1.4 copy-start.18
  117.6 1.3 copy-start.17
  127.5 1.5 copy-start.16
  159.1 15.5 %all-to-all-start.5 = ((f32[128,1,256]{2,1,0:T(1,128)}), f32[128,1,256]{2,1,0:T(1,128)S(1)}, u32[]{:S(2)}, u32[]{:S(2)}) async-start(f32[128,1,256]{2,1,0:T(1,128)} %reshape.824), calls=%async_computation.5 | async-start | bytes 262144 | tf_op jit(solution)/shard_map/all_to_all | solution.py:124
  174.6 14.1 %all-to-all-start.4 = ((f32[128,1,256]{2,1,0:T(1,128)}), f32[128,1,256]{2,1,0:T(1,128)S(1)}, u32[]{:S(2)}, u32[]{:S(2)}) async-start(f32[128,1,256]{2,1,0:T(1,128)} %reshape.822), calls=%async_computation.4 | async-start | bytes 262144 | tf_op jit(solution)/shard_map/all_to_all | solution.py:123
  193.8 1.6 copy-start.22
  193.8 1.6 copy-start.24
  208.0 14.1 %all-to-all-start.7 = ((f32[128,1,256]{2,1,0:T(1,128)}), f32[128,1,256]{2,1,0:T(1,128)S(1)}, u32[]{:S(2)}, u32[]{:S(2)}) async-start(f32[128,1,256]{2,1,0:T(1,128)} %reshape.828), calls=%async_computation.7 | async-start | bytes 262144 | tf_op jit(solution)/shard_map/all_to_all | solution.py:136
  222.1 14.1 %all-to-all-start.6 = ((f32[128,1,256]{2,1,0:T(1,128)}), f32[128,1,256]{2,1,0:T(1,128)S(1)}, u32[]{:S(2)}, u32[]{:S(2)}) async-start(f32[128,1,256]{2,1,0:T(1,128)} %reshape.826), calls=%async_computation.6 | async-start | bytes 262144 | tf_op jit(solution)/shard_map/all_to_all | solution.py:135
  282.8 3.4 collective-permute-start.6
  283.4 2.8 collective-permute-start.7
  284.4 3.1 collective-permute-start.8
  285.3 2.2 collective-permute-start.9
  336.3 84.1 %copy-start.3 = (f32[128,16,16]{0,2,1:T(8,128)}, f32[128,16,16]{0,2,1:T(8,128)S(1)}, u32[]{:S(2)}) copy-start(f32[128,16,16]{0,2,1:T(8,128)S(1)} %multiply_subtract_fusion.2) | copy-start | bytes 393220
  338.4 14.9 %all-to-all-start.9 = ((f32[128,1,256]{2,1,0:T(1,128)}), f32[128,1,256]{2,1,0:T(1,128)S(1)}, u32[]{:S(2)}, u32[]{:S(2)}) async-start(f32[128,1,256]{2,1,0:T(1,128)} %reshape.832), calls=%async_computation.9 | async-start | bytes 262144 | tf_op jit(solution)/shard_map/all_to_all | solution.py:124
  353.3 14.9 %all-to-all-start.8 = ((f32[128,1,256]{2,1,0:T(1,128)}), f32[128,1,256]{2,1,0:T(1,128)}, u32[]{:S(2)}, u32[]{:S(2)}) async-start(f32[128,1,256]{2,1,0:T(1,128)} %reshape.830), calls=%async_computation.8 | async-start | bytes 262144 | tf_op jit(solution)/shard_map/all_to_all | solution.py:123
  371.0 0.9 copy-start.14
  383.5 0.6 copy-start.8
  389.5 6.7 copy-start.9
  389.5 6.7 copy-start.12
  389.5 14.7 %all-to-all-start.11 = ((f32[128,1,256]{2,1,0:T(1,128)}), f32[128,1,256]{2,1,0:T(1,128)S(1)}, u32[]{:S(2)}, u32[]{:S(2)}) async-start(f32[128,1,256]{2,1,0:T(1,128)} %reshape.836), calls=%async_computation.11 | async-start | bytes 262144 | tf_op jit(solution)/shard_map/all_to_all | solution.py:136
  404.2 14.1 %all-to-all-start.10 = ((f32[128,1,256]{2,1,0:T(1,128)}), f32[128,1,256]{2,1,0:T(1,128)S(1)}, u32[]{:S(2)}, u32[]{:S(2)}) async-start(f32[128,1,256]{2,1,0:T(1,128)} %reshape.834), calls=%async_computation.10 | async-start | bytes 262144 | tf_op jit(solution)/shard_map/all_to_all | solution.py:135
  464.8 3.4 collective-permute-start.10
  465.5 2.8 collective-permute-start.11
  466.4 3.1 collective-permute-start.12
  467.3 2.2 collective-permute-start.13
  469.5 48.9 %copy-start.4 = (f32[128,16,16]{0,2,1:T(8,128)S(1)}, f32[128,16,16]{0,2,1:T(8,128)}, u32[]{:S(2)}) copy-start(f32[128,16,16]{0,2,1:T(8,128)} %copy-done.3) | copy-start | bytes 393220
  520.4 14.9 %all-to-all-start.13 = ((f32[128,1,256]{2,1,0:T(1,128)}), f32[128,1,256]{2,1,0:T(1,128)S(1)}, u32[]{:S(2)}, u32[]{:S(2)}) async-start(f32[128,1,256]{2,1,0:T(1,128)} %reshape.840), calls=%async_computation.13 | async-start | bytes 262144 | tf_op jit(solution)/shard_map/all_to_all | solution.py:124
  535.3 14.9 %all-to-all-start.12 = ((f32[128,1,256]{2,1,0:T(1,128)}), f32[128,1,256]{2,1,0:T(1,128)}, u32[]{:S(2)}, u32[]{:S(2)}) async-start(f32[128,1,256]{2,1,0:T(1,128)} %reshape.838), calls=%async_computation.12 | async-start | bytes 262144 | tf_op jit(solution)/shard_map/all_to_all | solution.py:123
  544.7 1.2 copy-start.5
  553.1 0.9 copy-start.15
  554.5 1.6 copy-start.6
  565.5 0.7 copy-start.10
  571.3 7.8 %copy-start.11 = (f32[128,256]{0,1:T(8,128)S(1)}, f32[128,256]{0,1:T(8,128)}, u32[]{:S(2)}) copy-start(f32[128,256]{0,1:T(8,128)} %copy-done.10) | copy-start | bytes 393220
  571.3 7.8 %copy-start.13 = (f32[128,256]{1,0:T(8,128)S(1)}, f32[128,256]{1,0:T(8,128)}, u32[]{:S(2)}) copy-start(f32[128,256]{1,0:T(8,128)} %fusion.188) | copy-start | bytes 393220
  571.3 15.4 %all-to-all-start.15 = ((f32[128,1,256]{2,1,0:T(1,128)}), f32[128,1,256]{2,1,0:T(1,128)}, u32[]{:S(2)}, u32[]{:S(2)}) async-start(f32[128,1,256]{2,1,0:T(1,128)} %reshape.844), calls=%async_computation.15 | async-start | bytes 262144 | tf_op jit(solution)/shard_map/all_to_all | solution.py:136
  586.7 14.4 %all-to-all-start.14 = ((f32[128,1,256]{2,1,0:T(1,128)}), f32[128,1,256]{2,1,0:T(1,128)S(1)}, u32[]{:S(2)}, u32[]{:S(2)}) async-start(f32[128,1,256]{2,1,0:T(1,128)} %reshape.842), calls=%async_computation.14 | async-start | bytes 262144 | tf_op jit(solution)/shard_map/all_to_all | solution.py:135
  647.7 3.4 collective-permute-start.14
  648.3 2.8 collective-permute-start.15
  649.2 3.1 collective-permute-start.16
  650.1 2.2 collective-permute-start.17
